TPU v7x, 256 devices: a whole 4x4x8 slice. The times are simulated.
256 devices in a mesh: unit: 4 (over x), north: 4 (over y), east: 16 (over z, core).
Axes of the slice: x: 4, y: 4, z: 8, core: 2. Of those that a mesh axis runs over, the one named last changes fastest.
Arguments:
- pair_rows: bfloat16 [2048, 512, 128], P(('unit', 'north'), 'east'), parts along dimension 0, may hold values from -6 to 6
- in_gain: float32 [128], replicated, may hold values from 0.25 to 1.75
- left_weight: bfloat16 [512, 128], P('unit'), parts along dimension 0, may hold values from -0.5 to 0.5
- right_weight: bfloat16 [512, 128], P('unit'), parts along dimension 0, may hold values from -0.5 to 0.5
- left_gate: bfloat16 [512, 128], P('unit'), parts along dimension 0, may hold values from -0.5 to 0.5
- right_gate: bfloat16 [512, 128], P('unit'), parts along dimension 0, may hold values from -0.5 to 0.5
- mid_gain: float32 [128], replicated, may hold values from 0.25 to 1.75
- out_weight: bfloat16 [512, 128], P('unit'), parts along dimension 0, may hold values from -0.5 to 0.5
- out_gate: bfloat16 [512, 128], P('unit'), parts along dimension 0, may hold values from -0.5 to 0.5
Outputs:
- triangle_out: bfloat16 [2048, 512, 128], P(('unit', 'north'), 'east'), parts along dimension 0
There are 4 independent parts, one for each index of `unit`. A program takes and returns all parts, laid end to end along the dimension named above; an argument that names none is the same for every part. Nothing has to cross between parts.
All inputs are finite; a program needn't handle non-finite values.
Results may differ from a plain program's by a relative error of at most 0.015.
Values may be sent and summed in bfloat16 or wider, within the bound.
A program may use at most 128 MiB of HBM per device.

v0:
```python
import jax
import jax.numpy as jnp
from jax import lax
from jax.sharding import PartitionSpec as P


def over_all(piece, axis, dim, apply):
    everything = lax.all_gather(piece, axis, axis=dim, tiled=True)
    return apply(everything, jnp.int32(0))


def scale_channels(values, channel_gain):
    centred = values - jnp.mean(values, axis=-1, keepdims=True)
    return (
        centred
        * lax.rsqrt(jnp.mean(centred * centred, axis=-1, keepdims=True) + 1e-05)
        * channel_gain
    )


def make_factors(pair_in, in_gain, left_weight, right_weight, left_gate, right_gate):
    ready = scale_channels(pair_in.astype(jnp.float32), in_gain).astype(jnp.bfloat16)
    ready = lax.optimization_barrier(ready)
    left = jnp.einsum("ijc,cd->ijd", ready, left_weight, preferred_element_type=jnp.float32)
    left = left * jax.nn.sigmoid(
        jnp.einsum("ijc,cd->ijd", ready, left_gate, preferred_element_type=jnp.float32)
    )
    right = jnp.einsum("ijc,cd->ijd", ready, right_weight, preferred_element_type=jnp.float32)
    right = right * jax.nn.sigmoid(
        jnp.einsum("ijc,cd->ijd", ready, right_gate, preferred_element_type=jnp.float32)
    )
    return (ready, left.astype(jnp.bfloat16), right.astype(jnp.bfloat16))


def finish_pair(mixed, ready, mid_gain, out_weight, out_gate):
    scaled = scale_channels(mixed.astype(jnp.float32), mid_gain).astype(jnp.bfloat16)
    scaled = lax.optimization_barrier(scaled)
    gate = jax.nn.sigmoid(
        jnp.einsum("ijc,cd->ijd", ready, out_gate, preferred_element_type=jnp.float32)
    )
    return (
        jnp.einsum("ijd,dc->ijc", scaled, out_weight, preferred_element_type=jnp.float32) * gate
    ).astype(jnp.bfloat16)


def body(
    pair_rows,
    in_gain,
    left_weight,
    right_weight,
    left_gate,
    right_gate,
    mid_gain,
    out_weight,
    out_gate,
):
    ready, left, right = make_factors(
        pair_rows, in_gain, left_weight, right_weight, left_gate, right_gate
    )
    count = pair_rows.shape[0] * lax.axis_size("north")
    left_lines, right_lines = (
        lax.all_to_all(left, "north", split_axis=2, concat_axis=0, tiled=True),
        lax.all_to_all(right, "north", split_axis=2, concat_axis=0, tiled=True),
    )

    def meet(piece, start):
        return jnp.einsum("kid,kjd->ijd", piece, right_lines, preferred_element_type=jnp.float32)

    strip = over_all(left_lines, "east", 1, meet)
    strip = (strip * count ** (-0.5)).astype(jnp.bfloat16)
    mixed = lax.all_to_all(strip, "north", split_axis=0, concat_axis=2, tiled=True)
    return finish_pair(mixed, ready, mid_gain, out_weight, out_gate)


def solution(mesh):
    placed = (
        P(("unit", "north"), "east", None),
        P(),
        P("unit", None),
        P("unit", None),
        P("unit", None),
        P("unit", None),
        P(),
        P("unit", None),
        P("unit", None),
    )
    return jax.shard_map(
        body,
        mesh=mesh,
        in_specs=placed,
        out_specs=P(("unit", "north"), "east", None),
        check_vma=False,
    )
```

profile of v0, /device:TPU:7, one launch (start us, length us, event | category | flops | bytes accessed | tf_op | source)
XLA Modules:
  0.0 197.9 jit_solution(17463948543864355809)
XLA Ops:
  6.5 1.9 convert_reduce_fusion
  8.7 2.3 %fusion.2 = f32[128,32]{1,0:T(8,128)S(1)} fusion(bf16[128,32,128]{2,1,0:T(8,128)(2,1)} %param.9, f32[128,32]{1,0:T(8,128)S(1)} %copy.94), kind=kLoop, calls=%fused_computation.4 | loop fusion | flops 2093056 | bytes 1081344 | tf_op jit(solution)/shard_map/reduce_sum | solution.py:16
  11.2 1.5 fusion.4
  12.7 0.5 fusion.13
  13.3 0.2 copy-done.6
  13.5 1.0 multiply_convert_fusion.2
  14.5 1.0 copy.104
  15.5 18.2 %all_to_all.45 = bf16[128,32,128]{0,1,2:T(8,128)(2,1)S(1)} all-to-all(bf16[128,32,128]{0,1,2:T(8,128)(2,1)S(1)} %copy.104), channel_id=1, replica_groups=mesh['unit'=4,'north'=4,'east'=16] {'north'}, dimensions={2} | all-to-all | bytes 2097152 | tf_op jit(solution)/shard_map/all_to_all | solution.py:62
  33.7 1.3 copy.133
  35.0 0.5 fusion.16
  35.5 0.2 copy-done.7
  35.7 1.0 multiply_convert_fusion.3
  36.8 1.0 copy.99
  37.7 15.8 %all_to_all.46 = bf16[128,32,128]{0,1,2:T(8,128)(2,1)S(1)} all-to-all(bf16[128,32,128]{0,1,2:T(8,128)(2,1)S(1)} %copy.99), channel_id=1, replica_groups=mesh['unit'=4,'north'=4,'east'=16] {'north'}, dimensions={2} | all-to-all | bytes 2097152 | tf_op jit(solution)/shard_map/all_to_all | solution.py:63
  53.5 79.3 %all-gather.2.cloned.1.call-done = bf16[512,512,32]{0,1,2:T(8,128)(2,1)} async-done(((bf16[512,32,32]{0,1,2:T(8,128)(2,1)}), bf16[512,512,32]{0,1,2:T(8,128)(2,1)}) %all-gather.2.cloned.1.call-update) | async-done | bytes 16777232 | tf_op jit(solution)/shard_map/all_gather | solution.py:8
  132.9 10.7 %fusion.8 = bf16[512,32,32]{0,1,2:T(8,128)(2,1)S(1)} fusion(bf16[512,512,32]{0,1,2:T(8,128)(2,1)} %all-gather.2.cloned.1.call-done, bf16[4,32,4,8,128]{4,3,2,1,0:T(8,128)(2,1)S(1)} %bitcast.54), kind=kOutput, calls=%fused_computation.16 | convolution fusion | flops 537919488 | bytes 18874368 | tf_op jit(solution)/shard_map/kid,kjd->ijd/dot_general | solution.py:67
  143.6 6.5 %copy.107 = bf16[512,32,32]{1,2,0:T(8,128)(2,1)} copy(bf16[512,32,32]{0,1,2:T(8,128)(2,1)S(1)} %fusion.8) | data formatting | bytes 2097152 | tf_op jit(solution)/shard_map/convert_element_type | solution.py:70
  150.0 5.6 %reshape.41 = bf16[4,2,65536]{2,1,0:T(2,128)(2,1)S(1)} reshape(bf16[512,32,32]{2,1,0:T(8,128)(2,1)} %bitcast.52) | data formatting | bytes 2097152
  155.6 18.5 %all_to_all.47 = bf16[4,2,65536]{2,1,0:T(2,128)(2,1)S(1)} all-to-all(bf16[4,2,65536]{2,1,0:T(2,128)(2,1)S(1)} %reshape.41), channel_id=1, replica_groups=mesh['unit'=4,'north'=4,'east'=16] {'north'}, dimensions={0} | all-to-all | bytes 2097152 | tf_op jit(solution)/shard_map/all_to_all | solution.py:71
  174.1 3.5 %reshape.42 = bf16[512,32,32]{2,1,0:T(8,128)(2,1)} reshape(bf16[4,2,65536]{2,1,0:T(2,128)(2,1)S(1)} %all_to_all.47) | data formatting | bytes 2097152
  177.6 6.0 %copy.108 = bf16[512,32,32]{0,2,1:T(8,128)(2,1)} copy(bf16[512,32,32]{1,2,0:T(8,128)(2,1)} %bitcast.53) | data formatting | bytes 2097152 | tf_op jit(solution)/shard_map/all_to_all | solution.py:71
  183.6 1.7 reshape.34
  185.4 0.2 bitcast_reduce_fusion
  185.6 0.6 multiply_reduce_fusion
  186.3 0.3 copy.109
  186.5 0.4 copy-done.5
  186.9 0.4 fusion.7
  187.4 0.3 copy-done.3
  187.7 0.5 fusion.19
  188.1 0.3 copy-done.8
  188.4 1.0 multiply_convert_fusion
  189.4 1.6 copy.112
  (23 shorter events, 0.4 us)
Async XLA Ops:
  6.5 6.2 %copy-start = (bf16[128,128]{1,0:T(8,128)(2,1)S(1)}, bf16[128,128]{1,0:T(8,128)(2,1)}, u32[]{:S(2)}) copy-start(bf16[128,128]{1,0:T(8,128)(2,1)} %param.11) | copy-start | bytes 98308
  6.5 4.6 %copy-start.1 = (bf16[128,32,128]{2,1,0:T(8,128)(2,1)S(1)}, bf16[128,32,128]{2,1,0:T(8,128)(2,1)}, u32[]{:S(2)}) copy-start(bf16[128,32,128]{2,1,0:T(8,128)(2,1)} %param.9) | copy-start | bytes 3145732
  6.5 4.6 %copy-start.4 = (f32[128]{0:T(128)S(1)}, f32[128]{0:T(128)}, u32[]{:S(2)}) copy-start(f32[128]{0:T(128)} %param.10) | copy-start | bytes 1540
  6.5 126.3 %all-gather.2.cloned.1.call-start = ((), (), s32[]{:S(2)}) async-start(), calls=%async_computation.3 | async-start | bytes 17825792 | tf_op jit(solution)/shard_map/all_gather | solution.py:8
  12.7 0.8 copy-start.6
  33.7 1.3 copy-start.2
  35.0 0.8 copy-start.7
  186.3 0.7 copy-start.5
  186.9 0.8 copy-start.3
  187.7 0.8 copy-start.8
Sparse Core Ops, SparseCore 0:
  35.1 97.6 all-gather.1
where the time goes:
time: 200 us; the launch traced here: 198 us
  waiting for transfers between devices  79.3 us (40%)
  blocking collectives  52.5 us (26%)
  local copies, waits for them, and re-layouts  30.2 us (15%)
  matrix products  15.2 us (8%)
  between operations  13.6 us (7%)
  other arithmetic  7.1 us (4%)
    all_gather x1, waiting for transfers between devices, over_all(): everything = lax.all_gather(piece, axis, axis=dim, tiled=True)  79.3 us
    all_to_all x1, blocking collectives, body(): lax.all_to_all(strip, 'north', split_axis=0, concat_axis=2, tiled=True)  18.5 us
    all_to_all x1, blocking collectives, body(): lax.all_to_all(left, 'north', split_axis=2, concat_axis=0, tiled=True)  18.2 us
    all_to_all x1, blocking collectives, body(): lax.all_to_all(right, 'north', split_axis=2, concat_axis=0, tiled=True)  15.8 us
    dot_general x1, matrix products, meet(): jnp.einsum('kid,kjd->ijd', piece, right_lines, preferred_element_type=jnp...  10.7 us
    unnamed x20, local copies, waits for them, and re-layouts  10.5 us
    convert_element_type x1, local copies, waits for them, and re-layouts, body(): strip = (strip * count ** (-0.5)).astype(jnp.bfloat16)  6.45 us
    all_to_all x1, local copies, waits for them, and re-layouts, body(): lax.all_to_all(strip, 'north', split_axis=0, concat_axis=2, tiled=True)  6.02 us
  transfers between devices with their start and end apart: 1, of which 1 were waited for; matrix products, arithmetic and copies ran while one was open for 1% of the time, Pallas kernels for 0%

commit v1 on v0

v1 whole, which is shorter than its diff:
```python
import jax
import jax.numpy as jnp
from jax import lax
from jax.experimental import pallas as pl
from jax.experimental.pallas import tpu as pltpu
from jax.sharding import PartitionSpec as P

MESH = pl.DeviceIdType.MESH
F32 = jnp.float32
BF16 = jnp.bfloat16
NT = (((1,), (1,)), ((), ()))

NORTH, EAST = 4, 16
PEERS = NORTH * EAST
ROWS, COLS, WIDTH = 128, 32, 128
LINES = NORTH * ROWS
S = 36


def logistic(v):
    return 0.5 * jnp.tanh(0.5 * v) + 0.5


def turned(w):
    return w.astype(F32).T.astype(BF16)


def column(gain_ref):
    return jnp.broadcast_to(gain_ref[...], (WIDTH, WIDTH)).T


def kernel(
    x_ref, in_gain, lw, rw, lg, rg, mid_gain, ow, og, o_ref,
    rows, xt, gate, stage, wt, owt, ogt, gin, gmid,
    send1, recv1, send2, recv2, ssem1, rsem1, ssem2, rsem2,
):
    n, e = lax.axis_index("north"), lax.axis_index("east")
    me = n * EAST + e

    def peer(s):
        t = s + 1
        return lax.rem(n + lax.rem(t, NORTH), NORTH), lax.rem(e + t // NORTH, EAST)

    def each(count, fn, unroll=1):
        def step(s, c):
            fn(s)
            return c

        lax.fori_loop(0, count, step, 0, unroll=unroll)

    barrier = pltpu.get_barrier_semaphore()

    def greet(s):
        n2, e2 = peer(s)
        pl.semaphore_signal(
            barrier, 1, device_id={"north": n2, "east": e2}, device_id_type=MESH
        )

    each(PEERS - 1, greet)

    for kind, w in enumerate((lw, lg, rw, rg)):
        t = turned(w[...])
        wt[0, kind], wt[1, kind] = t[:PEERS], t[PEERS:]
    owt[...] = turned(ow[...])
    ogt[...] = turned(og[...])
    gin[...] = column(in_gain)
    gmid[...] = column(mid_gain)

    def widen(k):
        rows[pl.ds(k * S, COLS), :] = x_ref[k].astype(F32)

    each(ROWS, widen, 4)

    def norm(i):
        v = rows[pl.ds(i, ROWS, stride=S), :].T
        v = v - jnp.mean(v, axis=0, keepdims=True)
        v = v * lax.rsqrt(jnp.mean(v * v, axis=0, keepdims=True) + 1e-05) * gin[...]
        xt[:, pl.ds(pl.multiple_of(i * ROWS, ROWS), ROWS)] = v.astype(BF16)

    each(COLS, norm, 2)

    def columns(i):
        return pl.ds(pl.multiple_of(i * 2 * ROWS, 2 * ROWS), 2 * ROWS)

    def project(h):
        def pair(i):
            y = jnp.dot(
                wt[h].reshape(4 * PEERS, WIDTH), xt[:, columns(i)], preferred_element_type=F32
            )
            for kind in range(2):
                base = kind * 2 * PEERS
                f = y[base : base + PEERS] * logistic(y[base + PEERS : base + 2 * PEERS])
                for t in range(2):
                    stage[pl.ds(kind * PEERS * S + 2 * i + t, PEERS, stride=S), :] = f[
                        :, t * ROWS : (t + 1) * ROWS
                    ]

        each(COLS // 2, pair)

        def pack(p):
            for kind in range(2):
                send1[h, p, kind] = stage[
                    pl.ds(kind * PEERS * S + p * S, COLS), :
                ].astype(BF16)

        each(PEERS, pack, 2)

    def home1(h, n2, e2):
        return recv1.at[
            h,
            :,
            pl.ds(pl.multiple_of(e2 * COLS, COLS), COLS),
            pl.ds(pl.multiple_of(n2 * ROWS, ROWS), ROWS),
        ]

    def give1(h):
        def go(s):
            n2, e2 = peer(s)
            pltpu.make_async_remote_copy(
                send1.at[h, n2 * EAST + e2],
                home1(h, n, e),
                ssem1.at[h],
                rsem1.at[h],
                device_id={"north": n2, "east": e2},
                device_id_type=MESH,
            ).start()

        each(PEERS - 1, go)
        home1(h, n, e)[...] = send1[h, me]

    def piece2(h, n2, e2):
        return send2.at[
            h,
            pl.ds(pl.multiple_of(e2 * COLS, COLS), COLS),
            pl.ds(pl.multiple_of(n2 * ROWS, ROWS), ROWS),
        ]

    def give2(h):
        def go(s):
            n2, e2 = peer(s)
            pltpu.make_async_remote_copy(
                piece2(h, n2, e2),
                recv2.at[h * PEERS + me],
                ssem2.at[h],
                rsem2.at[h],
                device_id={"north": n2, "east": e2},
                device_id_type=MESH,
            ).start()

        each(PEERS - 1, go)
        recv2[h * PEERS + me] = piece2(h, n, e)[...]

    def all1(h, sem):
        ref = send1.at[h, pl.ds(0, PEERS - 1)]
        pltpu.make_async_copy(ref, ref, sem.at[h]).wait()

    def all2(h, sem):
        ref = recv2.at[pl.ds(0, PEERS - 1)]
        pltpu.make_async_copy(ref, ref, sem.at[h]).wait()

    project(0)
    pl.semaphore_wait(barrier, PEERS - 1)
    give1(0)
    project(1)
    give1(1)

    def open_gate(i):
        y = jnp.dot(ogt[...], xt[:, columns(i)], preferred_element_type=F32)
        gate[:, columns(i)] = logistic(y)

    each(COLS // 2, open_gate)

    for h in range(2):
        all1(h, rsem1)
        for half in range(2):
            lines = pl.ds(half * (LINES // 2), LINES // 2)
            m = lax.dot_general(
                recv1[h, 1], recv1[h, 0, lines, :], NT, preferred_element_type=F32
            )
            send2[h, :, lines] = (m * LINES**-0.5).astype(BF16)
        give2(h)

    for h in range(2):
        all2(h, rsem2)

    half = COLS // 2
    for part in range(2):
        here = pl.ds(part * half, half)

        def add(d, c):
            return c + recv2[d, here, :].astype(F32)

        zero = jnp.zeros((half, ROWS), F32)
        mean = lax.fori_loop(0, WIDTH, add, zero, unroll=8) * (1.0 / WIDTH)

        def square(d, c):
            v = recv2[d, here, :].astype(F32) - mean
            return c + v * v

        scale = lax.rsqrt(
            lax.fori_loop(0, WIDTH, square, zero, unroll=8) * (1.0 / WIDTH) + 1e-05
        )

        def spread(d):
            v = (recv2[d, here, :].astype(F32) - mean) * scale
            stage[pl.ds(d * S + part * half, half), :] = v

        each(WIDTH, spread, 8)

    def finish(j):
        s = [
            (stage[pl.ds(2 * j + t, WIDTH, stride=S), :] * gmid[...]).astype(BF16)
            for t in range(2)
        ]
        y = jnp.dot(owt[...], jnp.concatenate(s, axis=1), preferred_element_type=F32)
        y = y * gate[:, columns(j)]
        for t in range(2):
            rows[pl.ds(2 * j + t, ROWS, stride=S), :] = y[:, t * ROWS : (t + 1) * ROWS].T

    each(COLS // 2, finish)

    def narrow(i):
        o_ref[i] = rows[pl.ds(i * S, COLS), :].astype(BF16)

    each(ROWS, narrow, 4)

    for h in range(2):
        all1(h, ssem1)
        all2(h, ssem2)


def body(x, in_gain, lw, rw, lg, rg, mid_gain, ow, og):
    vmem = pl.BlockSpec(memory_space=pltpu.VMEM)
    return pl.pallas_call(
        kernel,
        out_shape=jax.ShapeDtypeStruct(x.shape, BF16),
        in_specs=[vmem] * 9,
        out_specs=vmem,
        scratch_shapes=[
            pltpu.VMEM((ROWS * S, WIDTH), F32),
            pltpu.VMEM((WIDTH, COLS * ROWS), BF16),
            pltpu.VMEM((WIDTH, COLS * ROWS), F32),
            pltpu.VMEM((WIDTH * S, ROWS), F32),
            pltpu.VMEM((2, 4, PEERS, WIDTH), BF16),
            pltpu.VMEM((WIDTH, WIDTH), BF16),
            pltpu.VMEM((WIDTH, WIDTH), BF16),
            pltpu.VMEM((WIDTH, WIDTH), F32),
            pltpu.VMEM((WIDTH, WIDTH), F32),
            pltpu.VMEM((2, PEERS, 2, COLS, ROWS), BF16),
            pltpu.VMEM((2, 2, LINES, LINES), BF16),
            pltpu.VMEM((2, LINES, LINES), BF16),
            pltpu.VMEM((WIDTH, COLS, ROWS), BF16),
            pltpu.SemaphoreType.DMA((2,)),
            pltpu.SemaphoreType.DMA((2,)),
            pltpu.SemaphoreType.DMA((2,)),
            pltpu.SemaphoreType.DMA((2,)),
        ],
        compiler_params=pltpu.CompilerParams(
            collective_id=0, has_side_effects=True, vmem_limit_bytes=40 * 2**20
        ),
        name="triangle",
    )(x, in_gain.reshape(1, WIDTH), lw, rw, lg, rg, mid_gain.reshape(1, WIDTH), ow, og)


def solution(mesh):
    placed = (P(("unit", "north"), "east", None), P()) + (P("unit", None),) * 4
    placed += (P(),) + (P("unit", None),) * 2
    return jax.shard_map(
        body,
        mesh=mesh,
        in_specs=placed,
        out_specs=P(("unit", "north"), "east", None),
        check_vma=False,
    )
```

time: 200 us -> 103 us (0.52)
  Pallas kernels: 0 us -> 95.4 us
  waiting for transfers between devices: 79.3 us -> 0 us
  blocking collectives: 52.5 us -> 0 us
  local copies, waits for them, and re-layouts: 30.2 us -> 7.41 us
  matrix products: 15.2 us -> 0 us
  between operations: 13.6 us -> 0.02 us
  other arithmetic: 7.1 us -> 0 us
    pallas_call x0 -> x1, Pallas kernels: none -> 95.4 us  [body(): pl.pallas_call(kernel, out_shape=jax.ShapeDtypeStruct(x.shape, BF16), in_...]
    all_gather x1 -> x0, waiting for transfers between devices: 79.3 us -> none  [over_all(): everything = lax.all_gather(piece, axis, axis=dim, tiled=True)]
    all_to_all x3 -> x0, blocking collectives: 52.5 us -> none  [the longest x1 18.5 us: body(): lax.all_to_all(strip, 'north', split_axis=0, concat_axis=2, tiled=True)]
    dot_general x7 -> x0, matrix products: 15.2 us -> none  [the longest x1 10.7 us: meet(): jnp.einsum('kid,kjd->ijd', piece, right_lines, preferred_element_type=jnp...]
    convert_element_type x6 -> x0, local copies, waits for them, and re-layouts: 12 us -> none  [the longest x1 6.45 us: body(): strip = (strip * count ** (-0.5)).astype(jnp.bfloat16)]
    all_to_all x2 -> x0, local copies, waits for them, and re-layouts: 7.29 us -> none  [the longest x1 6.02 us: body(): lax.all_to_all(strip, 'north', split_axis=0, concat_axis=2, tiled=True)]
    reduce_sum x4 -> x0, other arithmetic: 5.09 us -> none  [the longest x2 2.94 us: scale_channels(): jnp.mean(centred * centred, axis=-1, keepdims=True) + 1e-05]
    unnamed x20 -> x19, local copies, waits for them, and re-layouts: 10.5 us -> 7.41 us
  transfers between devices with their start and end apart: 1 -> 0, of which waited for: 1 -> 0; matrix products, arithmetic and copies ran while one was open for 1% -> 0% of each run, Pallas kernels for 0% -> 0%
where the time goes in v1:
time: 103 us
  Pallas kernels  95.4 us (93%)
  local copies, waits for them, and re-layouts  7.41 us (7%)
    pallas_call x1, Pallas kernels, body(): pl.pallas_call(kernel, out_shape=jax.ShapeDtypeStruct(x.shape, BF16), in_...  95.4 us
    unnamed x19, local copies, waits for them, and re-layouts  7.41 us

profile of v1, /device:TPU:7, one launch (start us, length us, event | category | flops | bytes accessed | tf_op | source)
XLA Modules:
  0.0 102.8 jit_solution(3971117998881280120)
XLA Ops:
  0.0 0.0 copy-start.7
  0.0 0.0 copy-start.8
  0.0 0.7 copy-done.7
  0.7 0.0 copy-done.8
  0.7 0.0 copy-start
  0.7 1.2 %copy-done = bf16[128,32,128]{2,1,0:T(8,128)(2,1)S(1)} copy-done((bf16[128,32,128]{2,1,0:T(8,128)(2,1)S(1)}, bf16[128,32,128]{2,1,0:T(8,128)(2,1)}, u32[]{:S(2)}) %copy-start) | copy-done | bytes 1048600
  1.9 0.0 copy-start.1
  1.9 0.8 copy-done.1
  2.7 0.0 copy-start.2
  2.7 0.8 copy-done.2
  3.4 0.0 copy-start.3
  3.4 0.8 copy-done.3
  4.2 0.0 copy-start.4
  4.2 0.8 copy-done.4
  4.9 0.0 copy-start.5
  4.9 0.8 copy-done.5
  5.7 0.0 copy-start.6
  5.7 0.8 copy-done.6
  6.4 95.4 %triangle.1 = bf16[128,32,128]{2,1,0:T(8,128)(2,1)S(1)} custom-call(bf16[128,32,128]{2,1,0:T(8,128)(2,1)S(1)} %copy-done, f32[1,128]{1,0:T(1,128)S(1)} %bitcast.2, bf16[128,128]{1,0:T(8,128)(2,1)S(1)} %copy-done.1, bf16[128,128]{1,0:T(8,128)(2,1)S(1)} %copy-done.2, bf16[128,128]{1,0:T(8,128)(2,1)S(1)} %copy-done.3, bf16[128,128]{1,0:T(8,128)(2,1)S(1)} %copy-done.4, ...), custom_call_target="tpu_custom_call" | custom-call | tf_op jit(solution)/shard_map/triangle/pallas_call | solution.py:234
  101.9 1.0 copy.11
Async XLA Ops:
  0.0 0.7 copy-start.7
  0.0 0.7 copy-start.8
  0.7 1.2 %copy-start = (bf16[128,32,128]{2,1,0:T(8,128)(2,1)S(1)}, bf16[128,32,128]{2,1,0:T(8,128)(2,1)}, u32[]{:S(2)}) copy-start(bf16[128,32,128]{2,1,0:T(8,128)(2,1)} %x_ref.1) | copy-start | bytes 3145732
  1.9 0.8 copy-start.1
  2.7 0.8 copy-start.2
  3.4 0.8 copy-start.3
  4.2 0.8 copy-start.4
  4.9 0.8 copy-start.5
  5.7 0.8 copy-start.6

commit v2 on v1

v2 whole, which is shorter than its diff:
```python
import jax
import jax.numpy as jnp
from jax import lax
from jax.experimental import pallas as pl
from jax.experimental.pallas import tpu as pltpu
from jax.sharding import PartitionSpec as P

MESH = pl.DeviceIdType.MESH
F32 = jnp.float32
BF16 = jnp.bfloat16
NT = (((1,), (1,)), ((), ()))

NORTH, EAST = 4, 16
CHIPS, CORES = 8, 2
PEERS = NORTH * EAST
GROUP = PEERS // CORES
ROWS, COLS, WIDTH = 128, 32, 128
LINES = NORTH * ROWS
S = 36


def logistic(v):
    return 0.5 * jnp.tanh(0.5 * v) + 0.5


def turned(w):
    return w.astype(F32).T.astype(BF16)


def column(gain):
    return jnp.broadcast_to(gain, (WIDTH, WIDTH)).T


def kernel(
    x_hbm, in_gain_hbm, lw_hbm, rw_hbm, lg_hbm, rg_hbm, mid_gain_hbm, ow_hbm, og_hbm, o_ref,
    x_ref, weights, gains, rows, xt, gate, stage, wt, owt, ogt, gin, gmid,
    send1, recv1, send2, recv2, lsem, near, ssem1, rsem1, ssem2, rsem2,
):
    n, e = lax.axis_index("north"), lax.axis_index("east")
    z, core = e // CORES, lax.rem(e, CORES)

    def owner(n2, e2):
        return lax.rem(e2, CORES) * GROUP + n2 * CHIPS + e2 // CORES

    me = owner(n, e)

    def each(count, fn, unroll=1, start=0):
        def step(s, c):
            fn(s)
            return c

        lax.fori_loop(start, count, step, 0, unroll=unroll)

    loads = [pltpu.make_async_copy(x_hbm, x_ref, lsem.at[0])]
    for i, w in enumerate((lw_hbm, lg_hbm, rw_hbm, rg_hbm, ow_hbm, og_hbm)):
        loads.append(pltpu.make_async_copy(w, weights.at[i], lsem.at[1 + i]))
    for i, g in enumerate((in_gain_hbm, mid_gain_hbm)):
        loads.append(pltpu.make_async_copy(g, gains.at[i], lsem.at[7 + i]))
    for load in loads:
        load.start()

    barrier = pltpu.get_barrier_semaphore()

    def greet_row(s):
        pl.semaphore_signal(
            barrier,
            1,
            device_id={"north": n, "east": lax.rem(e + s, EAST)},
            device_id_type=MESH,
        )

    def greet_column(sem):
        def go(s):
            pl.semaphore_signal(
                sem,
                1,
                device_id={"north": lax.rem(n + s, NORTH), "east": e},
                device_id_type=MESH,
            )

        each(NORTH, go, start=1)

    each(EAST, greet_row, start=1)
    greet_column(barrier)
    for load in loads:
        load.wait()

    for kind in range(4):
        t = turned(weights[kind])
        for h in range(2):
            for c in range(CORES):
                first = h * PEERS + c * GROUP
                wt[h, c, kind] = t[first : first + GROUP]
    owt[...] = turned(weights[4])
    ogt[...] = turned(weights[5])
    gin[...] = column(gains[0])
    gmid[...] = column(gains[1])

    def widen(k):
        rows[pl.ds(k * S, COLS), :] = x_ref[k].astype(F32)

    each(ROWS, widen, 4)

    def norm(i):
        v = rows[pl.ds(i, ROWS, stride=S), :].T
        v = v - jnp.mean(v, axis=0, keepdims=True)
        v = v * lax.rsqrt(jnp.mean(v * v, axis=0, keepdims=True) + 1e-05) * gin[...]
        xt[:, pl.ds(pl.multiple_of(i * ROWS, ROWS), ROWS)] = v.astype(BF16)

    each(COLS, norm, 2)

    def columns(i):
        return pl.ds(pl.multiple_of(i * 2 * ROWS, 2 * ROWS), 2 * ROWS)

    def project(h, c):
        def pair(i):
            y = jnp.dot(
                wt[h, c].reshape(4 * GROUP, WIDTH), xt[:, columns(i)], preferred_element_type=F32
            )
            for kind in range(2):
                base = kind * 2 * GROUP
                f = y[base : base + GROUP] * logistic(y[base + GROUP : base + 2 * GROUP])
                for t in range(2):
                    stage[pl.ds(kind * GROUP * S + 2 * i + t, GROUP, stride=S), :] = f[
                        :, t * ROWS : (t + 1) * ROWS
                    ]

        each(COLS // 2, pair, 2)

        def pack(p):
            for kind in range(2):
                send1[h, c * GROUP + p, kind] = stage[
                    pl.ds((kind * GROUP + p) * S, COLS), :
                ].astype(BF16)

        each(GROUP, pack, 4)

    def home1(h, n2, e2):
        return recv1.at[
            h,
            :,
            pl.ds(pl.multiple_of(e2 * COLS, COLS), COLS),
            pl.ds(pl.multiple_of(n2 * ROWS, ROWS), ROWS),
        ]

    def give1(h, c):
        def go(s):
            n2 = lax.rem(n + lax.rem(s, NORTH), NORTH)
            e2 = lax.rem(z + s // NORTH, CHIPS) * CORES + c
            pltpu.make_async_remote_copy(
                send1.at[h, owner(n2, e2)],
                home1(h, n, e),
                ssem1.at[h],
                rsem1.at[h],
                device_id={"north": n2, "east": e2},
                device_id_type=MESH,
            ).start()

        each(GROUP, go, start=1 - lax.rem(c + core, CORES))

    def piece2(h, n2, e2, first, count):
        return send2.at[
            h,
            pl.ds(pl.multiple_of(e2 * COLS + first, count), count),
            pl.ds(pl.multiple_of(n2 * ROWS, ROWS), ROWS),
        ]

    def give2(h, turn, first, count):
        def go(s):
            n2 = lax.rem(n + lax.rem(s, NORTH), NORTH)
            e2 = lax.rem(e + s // NORTH, EAST)
            pltpu.make_async_remote_copy(
                piece2(h, n2, e2, first, count),
                recv2.at[h * PEERS + me, pl.ds(first, count)],
                ssem2.at[turn],
                rsem2.at[turn],
                device_id={"north": n2, "east": e2},
                device_id_type=MESH,
            ).start()

        each(PEERS, go, start=1)

    def all1(h, sem):
        ref = send1.at[h, pl.ds(0, PEERS - 1)]
        pltpu.make_async_copy(ref, ref, sem.at[h]).wait()

    def all2(turn, sem):
        ref = recv2.at[pl.ds(0, PEERS - 1), pl.ds(0, COLS if turn == 0 else COLS // 2)]
        pltpu.make_async_copy(ref, ref, sem.at[turn]).wait()

    project(0, 0)
    pl.semaphore_wait(barrier, EAST - 1 + NORTH - 1)
    greet_column(near)
    pl.semaphore_wait(near, NORTH - 1)
    give1(0, 0)
    project(0, 1)
    give1(0, 1)
    project(1, 0)
    give1(1, 0)
    project(1, 1)
    give1(1, 1)
    for h in range(2):
        home1(h, n, e)[...] = send1[h, me]

    def open_gate(i):
        y = jnp.dot(ogt[...], xt[:, columns(i)], preferred_element_type=F32)
        gate[:, columns(i)] = logistic(y)

    each(COLS // 2, open_gate)

    for h in range(2):
        all1(h, rsem1)
        for half in range(2):
            lines = pl.ds(half * (LINES // 2), LINES // 2)
            m = lax.dot_general(
                recv1[h, 1], recv1[h, 0, lines, :], NT, preferred_element_type=F32
            )
            send2[h, :, lines] = (m * LINES**-0.5).astype(BF16)
        recv2[h * PEERS + me] = piece2(h, n, e, 0, COLS)[...]
        if h == 0:
            give2(0, 0, 0, COLS)
        else:
            give2(1, 1, 0, COLS // 2)
            give2(1, 2, COLS // 2, COLS // 2)

    half = COLS // 2
    all2(0, rsem2)
    for part in range(2):
        all2(1 + part, rsem2)
        here = pl.ds(part * half, half)

        def add(d, c):
            return c + recv2[d, here, :].astype(F32)

        zero = jnp.zeros((half, ROWS), F32)
        mean = lax.fori_loop(0, WIDTH, add, zero, unroll=8) * (1.0 / WIDTH)

        def square(d, c):
            v = recv2[d, here, :].astype(F32) - mean
            return c + v * v

        scale = lax.rsqrt(
            lax.fori_loop(0, WIDTH, square, zero, unroll=8) * (1.0 / WIDTH) + 1e-05
        )

        def spread(d):
            v = (recv2[d, here, :].astype(F32) - mean) * scale
            stage[pl.ds(d * S + part * half, half), :] = v

        each(WIDTH, spread, 8)

        def finish(jj):
            j = part * (half // 2) + jj
            s = [
                (stage[pl.ds(2 * j + t, WIDTH, stride=S), :] * gmid[...]).astype(BF16)
                for t in range(2)
            ]
            y = jnp.dot(owt[...], jnp.concatenate(s, axis=1), preferred_element_type=F32)
            y = y * gate[:, columns(j)]
            for t in range(2):
                rows[pl.ds(2 * j + t, ROWS, stride=S), :] = y[:, t * ROWS : (t + 1) * ROWS].T

        each(half // 2, finish, 2)

        def narrow(i):
            o_ref[i, here, :] = rows[pl.ds(i * S + part * half, half), :].astype(BF16)

        each(ROWS, narrow, 8)

    for h in range(2):
        all1(h, ssem1)
    for turn in range(3):
        all2(turn, ssem2)


def body(x, in_gain, lw, rw, lg, rg, mid_gain, ow, og):
    vmem = pl.BlockSpec(memory_space=pltpu.VMEM)
    hbm = pl.BlockSpec(memory_space=pltpu.HBM)
    return pl.pallas_call(
        kernel,
        out_shape=jax.ShapeDtypeStruct(x.shape, BF16),
        in_specs=[hbm] * 9,
        out_specs=vmem,
        scratch_shapes=[
            pltpu.VMEM(x.shape, BF16),
            pltpu.VMEM((6, WIDTH, WIDTH), BF16),
            pltpu.VMEM((2, 1, WIDTH), F32),
            pltpu.VMEM((ROWS * S, WIDTH), F32),
            pltpu.VMEM((WIDTH, COLS * ROWS), BF16),
            pltpu.VMEM((WIDTH, COLS * ROWS), F32),
            pltpu.VMEM((WIDTH * S, ROWS), F32),
            pltpu.VMEM((2, CORES, 4, GROUP, WIDTH), BF16),
            pltpu.VMEM((WIDTH, WIDTH), BF16),
            pltpu.VMEM((WIDTH, WIDTH), BF16),
            pltpu.VMEM((WIDTH, WIDTH), F32),
            pltpu.VMEM((WIDTH, WIDTH), F32),
            pltpu.VMEM((2, PEERS, 2, COLS, ROWS), BF16),
            pltpu.VMEM((2, 2, LINES, LINES), BF16),
            pltpu.VMEM((2, LINES, LINES), BF16),
            pltpu.VMEM((WIDTH, COLS, ROWS), BF16),
            pltpu.SemaphoreType.DMA((9,)),
            pltpu.SemaphoreType.REGULAR,
            pltpu.SemaphoreType.DMA((2,)),
            pltpu.SemaphoreType.DMA((2,)),
            pltpu.SemaphoreType.DMA((3,)),
            pltpu.SemaphoreType.DMA((3,)),
        ],
        compiler_params=pltpu.CompilerParams(
            collective_id=0, has_side_effects=True, vmem_limit_bytes=40 * 2**20
        ),
        name="triangle",
    )(x, in_gain.reshape(1, WIDTH), lw, rw, lg, rg, mid_gain.reshape(1, WIDTH), ow, og)


def solution(mesh):
    placed = (P(("unit", "north"), "east", None), P()) + (P("unit", None),) * 4
    placed += (P(),) + (P("unit", None),) * 2
    return jax.shard_map(
        body,
        mesh=mesh,
        in_specs=placed,
        out_specs=P(("unit", "north"), "east", None),
        check_vma=False,
    )
```

time: 103 us -> 94.8 us (0.920)
  Pallas kernels: 95.4 us -> 86.8 us
    pallas_call x1, Pallas kernels: 95.4 us -> 86.8 us  [body(): pl.pallas_call(kernel, out_shape=jax.ShapeDtypeStruct(x.shape, BF16), in_...]
where the time goes in v2:
time: 94.8 us; the launch traced here: 94.3 us
  Pallas kernels  86.8 us (92%)
  local copies, waits for them, and re-layouts  7.41 us (8%)
    pallas_call x1, Pallas kernels, body(): pl.pallas_call(kernel, out_shape=jax.ShapeDtypeStruct(x.shape, BF16), in_...  86.8 us
    unnamed x19, local copies, waits for them, and re-layouts  7.41 us

profile of v2, /device:TPU:7, one launch (start us, length us, event | category | flops | bytes accessed | tf_op | source)
XLA Modules:
  0.0 94.3 jit_solution(12500917140787295344)
XLA Ops:
  0.0 0.0 copy-start.7
  0.0 0.0 copy-start.8
  0.0 0.7 copy-done.7
  0.7 0.0 copy-done.8
  0.7 0.0 copy-start
  0.7 1.2 %copy-done = bf16[128,32,128]{2,1,0:T(8,128)(2,1)S(1)} copy-done((bf16[128,32,128]{2,1,0:T(8,128)(2,1)S(1)}, bf16[128,32,128]{2,1,0:T(8,128)(2,1)}, u32[]{:S(2)}) %copy-start) | copy-done | bytes 1048600
  1.9 0.0 copy-start.1
  1.9 0.8 copy-done.1
  2.7 0.0 copy-start.2
  2.7 0.8 copy-done.2
  3.4 0.0 copy-start.3
  3.4 0.8 copy-done.3
  4.2 0.0 copy-start.4
  4.2 0.8 copy-done.4
  4.9 0.0 copy-start.5
  4.9 0.8 copy-done.5
  5.7 0.0 copy-start.6
  5.7 0.8 copy-done.6
  6.4 86.8 %triangle.1 = bf16[128,32,128]{2,1,0:T(8,128)(2,1)S(1)} custom-call(bf16[128,32,128]{2,1,0:T(8,128)(2,1)S(1)} %copy-done, f32[1,128]{1,0:T(1,128)S(1)} %bitcast.2, bf16[128,128]{1,0:T(8,128)(2,1)S(1)} %copy-done.1, bf16[128,128]{1,0:T(8,128)(2,1)S(1)} %copy-done.2, bf16[128,128]{1,0:T(8,128)(2,1)S(1)} %copy-done.3, bf16[128,128]{1,0:T(8,128)(2,1)S(1)} %copy-done.4, ...), custom_call_target="tpu_custom_call" | custom-call | tf_op jit(solution)/shard_map/triangle/pallas_call | solution.py:279
  93.3 1.0 %copy.11 = bf16[128,32,128]{2,1,0:T(8,128)(2,1)} copy(bf16[128,32,128]{2,1,0:T(8,128)(2,1)S(1)} %triangle.1) | data formatting | bytes 2097152
Async XLA Ops:
  0.0 0.7 copy-start.7
  0.0 0.7 copy-start.8
  0.7 1.2 %copy-start = (bf16[128,32,128]{2,1,0:T(8,128)(2,1)S(1)}, bf16[128,32,128]{2,1,0:T(8,128)(2,1)}, u32[]{:S(2)}) copy-start(bf16[128,32,128]{2,1,0:T(8,128)(2,1)} %x_hbm.1) | copy-start | bytes 3145732
  1.9 0.8 copy-start.1
  2.7 0.8 copy-start.2
  3.4 0.8 copy-start.3
  4.2 0.8 copy-start.4
  4.9 0.8 copy-start.5
  5.7 0.8 copy-start.6

commit v3 on v2

--- a/solution.py
+++ b/solution.py
@@ -34,7 +34,7 @@
 def kernel(
     x_hbm, in_gain_hbm, lw_hbm, rw_hbm, lg_hbm, rg_hbm, mid_gain_hbm, ow_hbm, og_hbm, o_ref,
     x_ref, weights, gains, rows, xt, gate, stage, wt, owt, ogt, gin, gmid,
-    send1, recv1, send2, recv2, lsem, near, ssem1, rsem1, ssem2, rsem2,
+    send1, recv1, send2, recv2, lsem, ssem1, rsem1, ssem2, rsem2,
 ):
     n, e = lax.axis_index("north"), lax.axis_index("east")
     z, core = e // CORES, lax.rem(e, CORES)
@@ -61,27 +61,14 @@
 
     barrier = pltpu.get_barrier_semaphore()
 
-    def greet_row(s):
+    def greet(s):
+        n2 = lax.rem(n + lax.rem(s, NORTH), NORTH)
+        e2 = lax.rem(e + s // NORTH, EAST)
         pl.semaphore_signal(
-            barrier,
-            1,
-            device_id={"north": n, "east": lax.rem(e + s, EAST)},
-            device_id_type=MESH,
+            barrier, 1, device_id={"north": n2, "east": e2}, device_id_type=MESH
         )
 
-    def greet_column(sem):
-        def go(s):
-            pl.semaphore_signal(
-                sem,
-                1,
-                device_id={"north": lax.rem(n + s, NORTH), "east": e},
-                device_id_type=MESH,
-            )
-
-        each(NORTH, go, start=1)
-
-    each(EAST, greet_row, start=1)
-    greet_column(barrier)
+    each(PEERS, greet, start=1)
     for load in loads:
         load.wait()
 
@@ -189,9 +176,7 @@
         pltpu.make_async_copy(ref, ref, sem.at[turn]).wait()
 
     project(0, 0)
-    pl.semaphore_wait(barrier, EAST - 1 + NORTH - 1)
-    greet_column(near)
-    pl.semaphore_wait(near, NORTH - 1)
+    pl.semaphore_wait(barrier, PEERS - 1)
     give1(0, 0)
     project(0, 1)
     give1(0, 1)
@@ -299,14 +284,13 @@
             pltpu.VMEM((2, LINES, LINES), BF16),
             pltpu.VMEM((WIDTH, COLS, ROWS), BF16),
             pltpu.SemaphoreType.DMA((9,)),
-            pltpu.SemaphoreType.REGULAR,
             pltpu.SemaphoreType.DMA((2,)),
             pltpu.SemaphoreType.DMA((2,)),
             pltpu.SemaphoreType.DMA((3,)),
             pltpu.SemaphoreType.DMA((3,)),
         ],
         compiler_params=pltpu.CompilerParams(
-            collective_id=0, has_side_effects=True, vmem_limit_bytes=40 * 2**20
+            collective_id=0, has_side_effects=True, vmem_limit_bytes=64_000_000
         ),
         name="triangle",
     )(x, in_gain.reshape(1, WIDTH), lw, rw, lg, rg, mid_gain.reshape(1, WIDTH), ow, og)

time: 94.8 us -> 91.8 us (0.968); the launches traced: 94.3 us -> 90.2 us
  local copies, waits for them, and re-layouts: 7.41 us -> 2.26 us
  Pallas kernels: 86.8 us -> 88 us
    unnamed x19 -> x1, local copies, waits for them, and re-layouts: 7.41 us -> 2.26 us
    pallas_call x1, Pallas kernels: 86.8 us -> 88 us  [body(): pl.pallas_call(kernel, out_shape=jax.ShapeDtypeStruct(x.shape, BF16), in_...]
where the time goes in v3:
time: 91.8 us; the launch traced here: 90.2 us
  Pallas kernels  88 us (96%)
  local copies, waits for them, and re-layouts  2.26 us (2%)
    pallas_call x1, Pallas kernels, body(): pl.pallas_call(kernel, out_shape=jax.ShapeDtypeStruct(x.shape, BF16), in_...  88 us
    unnamed x1, local copies, waits for them, and re-layouts  2.26 us

profile of v3, /device:TPU:7, one launch (start us, length us, event | category | flops | bytes accessed | tf_op | source)
XLA Modules:
  0.0 90.2 jit_solution(11779110483924007794)
XLA Ops:
  0.0 88.0 %triangle.1 = bf16[128,32,128]{2,1,0:T(8,128)(2,1)} custom-call(bf16[128,32,128]{2,1,0:T(8,128)(2,1)} %x_hbm.1, f32[1,128]{1,0:T(1,128)} %bitcast.2, bf16[128,128]{1,0:T(8,128)(2,1)} %lw_hbm.1, bf16[128,128]{1,0:T(8,128)(2,1)} %rw_hbm.1, bf16[128,128]{1,0:T(8,128)(2,1)} %lg_hbm.1, bf16[128,128]{1,0:T(8,128)(2,1)} %rg_hbm.1, f32[1,128]{1,0:T(1,128)} %bitcast.3, ...), custom_call_target="tpu_custom_call" | custom-call | tf_op jit(solution)/shard_map/triangle/pallas_call | solution.py:264
  88.0 2.3 %copy.11 = bf16[128,32,128]{2,1,0:T(8,128)(2,1)} copy(bf16[128,32,128]{2,1,0:T(8,128)(2,1)} %triangle.1) | data formatting | bytes 2097152

commit v4 on v3

--- a/solution.py
+++ b/solution.py
@@ -14,8 +14,10 @@
 CHIPS, CORES = 8, 2
 PEERS = NORTH * EAST
 GROUP = PEERS // CORES
+REACH = 4
 ROWS, COLS, WIDTH = 128, 32, 128
 LINES = NORTH * ROWS
+BAND = CORES * COLS
 S = 36
 
 
@@ -34,15 +36,16 @@
 def kernel(
     x_hbm, in_gain_hbm, lw_hbm, rw_hbm, lg_hbm, rg_hbm, mid_gain_hbm, ow_hbm, og_hbm, o_ref,
     x_ref, weights, gains, rows, xt, gate, stage, wt, owt, ogt, gin, gmid,
-    send1, recv1, send2, recv2, lsem, ssem1, rsem1, ssem2, rsem2,
+    send1, recv1, send2, recv2, lsem, ssem1, rsem1, ssemh, rsemh, ssem2, rsem2,
 ):
     n, e = lax.axis_index("north"), lax.axis_index("east")
     z, core = e // CORES, lax.rem(e, CORES)
 
-    def owner(n2, e2):
-        return lax.rem(e2, CORES) * GROUP + n2 * CHIPS + e2 // CORES
-
-    me = owner(n, e)
+    def set_of(c, n2, z2, side):
+        return c * GROUP + n2 * CHIPS + lax.rem(z2 - side + CHIPS, CHIPS)
+
+    def away(side, steps):
+        return lax.rem(z + CHIPS + (2 * side - 1) * steps, CHIPS)
 
     def each(count, fn, unroll=1, start=0):
         def step(s, c):
@@ -61,14 +64,21 @@
 
     barrier = pltpu.get_barrier_semaphore()
 
+    peers = (2 * REACH - 1) * CORES * NORTH
+
     def greet(s):
-        n2 = lax.rem(n + lax.rem(s, NORTH), NORTH)
-        e2 = lax.rem(e + s // NORTH, EAST)
+        q = peers - 1 - s
+        far = q // (CORES * NORTH)
+        step = (far + 1) // 2 * (1 - 2 * lax.rem(far, 2))
+        e2 = lax.rem(z + CHIPS + step, CHIPS) * CORES + lax.rem(core + q // NORTH, CORES)
         pl.semaphore_signal(
-            barrier, 1, device_id={"north": n2, "east": e2}, device_id_type=MESH
+            barrier,
+            1,
+            device_id={"north": lax.rem(n + q, NORTH), "east": e2},
+            device_id_type=MESH,
         )
 
-    each(PEERS, greet, start=1)
+    each(peers - 1, greet)
     for load in loads:
         load.wait()
 
@@ -122,61 +132,85 @@
 
         each(GROUP, pack, 4)
 
-    def home1(h, n2, e2):
+    def place1(h, side):
         return recv1.at[
             h,
+            side,
             :,
-            pl.ds(pl.multiple_of(e2 * COLS, COLS), COLS),
+            pl.ds(pl.multiple_of(e * COLS, COLS), COLS),
+            pl.ds(pl.multiple_of(n * ROWS, ROWS), ROWS),
+        ]
+
+    def give1(h, c):
+        def go(s):
+            q = GROUP - 1 - s
+            side, n2, steps = lax.rem(q, 2), lax.rem(n + q // 2, NORTH), q // (2 * NORTH)
+            z2 = away(1 - side, steps)
+            pltpu.make_async_remote_copy(
+                send1.at[h, set_of(c, n2, z2, side)],
+                place1(h, side),
+                ssem1.at[h],
+                rsem1.at[h, side],
+                device_id={"north": n2, "east": z2 * CORES + c},
+                device_id_type=MESH,
+            ).start()
+
+        each(GROUP - 2 * (1 - lax.rem(c + core, CORES)), go)
+
+    def band(h, side, kind, steps):
+        first = pl.multiple_of(away(side, steps) * BAND, BAND)
+        return recv1.at[h, side, kind, pl.ds(first, BAND)]
+
+    def hand(h, side):
+        z2 = away(1 - side, 1)
+        for steps in range(REACH):
+            first = pl.multiple_of(away(side, steps) * BAND, BAND)
+            pltpu.make_async_remote_copy(
+                recv1.at[h, side, 0, pl.ds(first, BAND)],
+                recv1.at[h, 1 - side, 0, pl.ds(first, BAND)],
+                ssemh.at[h, side],
+                rsemh.at[h, 1 - side],
+                device_id={"north": n, "east": z2 * CORES + core},
+                device_id_type=MESH,
+            ).start()
+
+    def piece2(h, side, steps, c, n2, first, count):
+        return send2.at[
+            h,
+            side,
+            pl.ds(pl.multiple_of(steps * BAND + c * COLS + first, count), count),
             pl.ds(pl.multiple_of(n2 * ROWS, ROWS), ROWS),
         ]
 
-    def give1(h, c):
+    def give2(h, side, turn, first, count):
         def go(s):
-            n2 = lax.rem(n + lax.rem(s, NORTH), NORTH)
-            e2 = lax.rem(z + s // NORTH, CHIPS) * CORES + c
+            q = GROUP - 1 - s
+            n2, c, steps = lax.rem(n + q, NORTH), lax.rem(core + q // NORTH, CORES), q // 8
             pltpu.make_async_remote_copy(
-                send1.at[h, owner(n2, e2)],
-                home1(h, n, e),
-                ssem1.at[h],
-                rsem1.at[h],
-                device_id={"north": n2, "east": e2},
+                piece2(h, side, steps, c, n2, first, count),
+                recv2.at[h * PEERS + set_of(core, n, z, side), pl.ds(first, count)],
+                ssem2.at[turn],
+                rsem2.at[turn],
+                device_id={"north": n2, "east": away(side, steps) * CORES + c},
                 device_id_type=MESH,
             ).start()
 
-        each(GROUP, go, start=1 - lax.rem(c + core, CORES))
-
-    def piece2(h, n2, e2, first, count):
-        return send2.at[
-            h,
-            pl.ds(pl.multiple_of(e2 * COLS + first, count), count),
-            pl.ds(pl.multiple_of(n2 * ROWS, ROWS), ROWS),
-        ]
-
-    def give2(h, turn, first, count):
-        def go(s):
-            n2 = lax.rem(n + lax.rem(s, NORTH), NORTH)
-            e2 = lax.rem(e + s // NORTH, EAST)
-            pltpu.make_async_remote_copy(
-                piece2(h, n2, e2, first, count),
-                recv2.at[h * PEERS + me, pl.ds(first, count)],
-                ssem2.at[turn],
-                rsem2.at[turn],
-                device_id={"north": n2, "east": e2},
-                device_id_type=MESH,
-            ).start()
-
-        each(PEERS, go, start=1)
-
-    def all1(h, sem):
-        ref = send1.at[h, pl.ds(0, PEERS - 1)]
-        pltpu.make_async_copy(ref, ref, sem.at[h]).wait()
-
-    def all2(turn, sem):
-        ref = recv2.at[pl.ds(0, PEERS - 1), pl.ds(0, COLS if turn == 0 else COLS // 2)]
-        pltpu.make_async_copy(ref, ref, sem.at[turn]).wait()
+        each(GROUP - 1, go)
+
+    def wait_for(ref, sem):
+        pltpu.make_async_copy(ref, ref, sem).wait()
+
+    def sent1(h, count):
+        return send1.at[h, pl.ds(0, count)]
+
+    def handed(h):
+        return recv1.at[h, 0, 0, pl.ds(0, REACH * BAND)]
+
+    def sent2(turn):
+        return recv2.at[pl.ds(0, PEERS - 2), pl.ds(0, COLS if turn == 0 else COLS // 2)]
 
     project(0, 0)
-    pl.semaphore_wait(barrier, PEERS - 1)
+    pl.semaphore_wait(barrier, peers - 1)
     give1(0, 0)
     project(0, 1)
     give1(0, 1)
@@ -185,7 +219,8 @@
     project(1, 1)
     give1(1, 1)
     for h in range(2):
-        home1(h, n, e)[...] = send1[h, me]
+        for side in range(2):
+            place1(h, side)[...] = send1[h, set_of(core, n, z, side)]
 
     def open_gate(i):
         y = jnp.dot(ogt[...], xt[:, columns(i)], preferred_element_type=F32)
@@ -194,24 +229,34 @@
     each(COLS // 2, open_gate)
 
     for h in range(2):
-        all1(h, rsem1)
-        for half in range(2):
-            lines = pl.ds(half * (LINES // 2), LINES // 2)
-            m = lax.dot_general(
-                recv1[h, 1], recv1[h, 0, lines, :], NT, preferred_element_type=F32
-            )
-            send2[h, :, lines] = (m * LINES**-0.5).astype(BF16)
-        recv2[h * PEERS + me] = piece2(h, n, e, 0, COLS)[...]
-        if h == 0:
-            give2(0, 0, 0, COLS)
-        else:
-            give2(1, 1, 0, COLS // 2)
-            give2(1, 2, COLS // 2, COLS // 2)
+        for side in range(2):
+            wait_for(sent1(h, GROUP - 1), rsem1.at[h, side])
+            hand(h, side)
+
+    for h in range(2):
+        for side in range(2):
+            wait_for(handed(h), rsemh.at[h, side])
+            right = jnp.concatenate([band(h, side, 1, k)[...] for k in range(REACH)], axis=0)
+            for part in range(2):
+                lines = pl.ds(part * (LINES // 2), LINES // 2)
+                m = lax.dot_general(
+                    right, recv1[h, side, 0, lines, :], NT, preferred_element_type=F32
+                )
+                send2[h, side, :, lines] = (m * LINES**-0.5).astype(BF16)
+            recv2[h * PEERS + set_of(core, n, z, side)] = piece2(
+                h, side, 0, core, n, 0, COLS
+            )[...]
+            if h == 0:
+                give2(0, side, 0, 0, COLS)
+        if h == 1:
+            for part in range(2):
+                for side in range(2):
+                    give2(1, side, 1 + part, part * (COLS // 2), COLS // 2)
 
     half = COLS // 2
-    all2(0, rsem2)
+    wait_for(sent2(0), rsem2.at[0])
     for part in range(2):
-        all2(1 + part, rsem2)
+        wait_for(sent2(1 + part), rsem2.at[1 + part])
         here = pl.ds(part * half, half)
 
         def add(d, c):
@@ -253,9 +298,11 @@
         each(ROWS, narrow, 8)
 
     for h in range(2):
-        all1(h, ssem1)
+        wait_for(sent1(h, PEERS - 2), ssem1.at[h])
+        for side in range(2):
+            wait_for(handed(h), ssemh.at[h, side])
     for turn in range(3):
-        all2(turn, ssem2)
+        wait_for(sent2(turn), ssem2.at[turn])
 
 
 def body(x, in_gain, lw, rw, lg, rg, mid_gain, ow, og):
@@ -280,12 +327,14 @@
             pltpu.VMEM((WIDTH, WIDTH), F32),
             pltpu.VMEM((WIDTH, WIDTH), F32),
             pltpu.VMEM((2, PEERS, 2, COLS, ROWS), BF16),
-            pltpu.VMEM((2, 2, LINES, LINES), BF16),
-            pltpu.VMEM((2, LINES, LINES), BF16),
+            pltpu.VMEM((2, 2, 2, LINES, LINES), BF16),
+            pltpu.VMEM((2, 2, REACH * BAND, LINES), BF16),
             pltpu.VMEM((WIDTH, COLS, ROWS), BF16),
             pltpu.SemaphoreType.DMA((9,)),
             pltpu.SemaphoreType.DMA((2,)),
-            pltpu.SemaphoreType.DMA((2,)),
+            pltpu.SemaphoreType.DMA((2, 2)),
+            pltpu.SemaphoreType.DMA((2, 2)),
+            pltpu.SemaphoreType.DMA((2, 2)),
             pltpu.SemaphoreType.DMA((3,)),
             pltpu.SemaphoreType.DMA((3,)),
         ],

time: 91.8 us -> 83.6 us (0.911)
  Pallas kernels: 88 us -> 80.2 us
    pallas_call x1, Pallas kernels: 88 us -> 80.2 us  [body(): pl.pallas_call(kernel, out_shape=jax.ShapeDtypeStruct(x.shape, BF16), in_...]
where the time goes in v4:
time: 83.6 us; the launch traced here: 82.5 us
  Pallas kernels  80.2 us (96%)
  local copies, waits for them, and re-layouts  2.26 us (3%)
    pallas_call x1, Pallas kernels, body(): pl.pallas_call(kernel, out_shape=jax.ShapeDtypeStruct(x.shape, BF16), in_...  80.2 us
    unnamed x1, local copies, waits for them, and re-layouts  2.26 us

profile of v4, /device:TPU:7, one launch (start us, length us, event | category | flops | bytes accessed | tf_op | source)
XLA Modules:
  0.0 82.5 jit_solution(3828788872476267253)
XLA Ops:
  0.0 80.2 %triangle.1 = bf16[128,32,128]{2,1,0:T(8,128)(2,1)} custom-call(bf16[128,32,128]{2,1,0:T(8,128)(2,1)} %x_hbm.1, f32[1,128]{1,0:T(1,128)} %bitcast.2, bf16[128,128]{1,0:T(8,128)(2,1)} %lw_hbm.1, bf16[128,128]{1,0:T(8,128)(2,1)} %rw_hbm.1, bf16[128,128]{1,0:T(8,128)(2,1)} %lg_hbm.1, bf16[128,128]{1,0:T(8,128)(2,1)} %rg_hbm.1, f32[1,128]{1,0:T(1,128)} %bitcast.3, ...), custom_call_target="tpu_custom_call" | custom-call | tf_op jit(solution)/shard_map/triangle/pallas_call | solution.py:311
  80.2 2.3 %copy.11 = bf16[128,32,128]{2,1,0:T(8,128)(2,1)} copy(bf16[128,32,128]{2,1,0:T(8,128)(2,1)} %triangle.1) | data formatting | bytes 2097152

commit v5 on v4

--- a/solution.py
+++ b/solution.py
@@ -15,6 +15,7 @@
 PEERS = NORTH * EAST
 GROUP = PEERS // CORES
 REACH = 4
+PIECES = ((0, 16), (16, 8), (24, 8))
 ROWS, COLS, WIDTH = 128, 32, 128
 LINES = NORTH * ROWS
 BAND = CORES * COLS
@@ -36,7 +37,7 @@
 def kernel(
     x_hbm, in_gain_hbm, lw_hbm, rw_hbm, lg_hbm, rg_hbm, mid_gain_hbm, ow_hbm, og_hbm, o_ref,
     x_ref, weights, gains, rows, xt, gate, stage, wt, owt, ogt, gin, gmid,
-    send1, recv1, send2, recv2, lsem, ssem1, rsem1, ssemh, rsemh, ssem2, rsem2,
+    send1, recv1, send2, recv2, lsem, near, ssem1, rsem1, ssemh, rsemh, ssem2, rsem2,
 ):
     n, e = lax.axis_index("north"), lax.axis_index("east")
     z, core = e // CORES, lax.rem(e, CORES)
@@ -63,14 +64,14 @@
         load.start()
 
     barrier = pltpu.get_barrier_semaphore()
-
-    peers = (2 * REACH - 1) * CORES * NORTH
+    partner = {"north": n, "east": e + 1 - 2 * core}
+    peers = (2 * REACH - 1) * NORTH
 
     def greet(s):
         q = peers - 1 - s
-        far = q // (CORES * NORTH)
+        far = q // NORTH
         step = (far + 1) // 2 * (1 - 2 * lax.rem(far, 2))
-        e2 = lax.rem(z + CHIPS + step, CHIPS) * CORES + lax.rem(core + q // NORTH, CORES)
+        e2 = lax.rem(z + CHIPS + step, CHIPS) * CORES + core
         pl.semaphore_signal(
             barrier,
             1,
@@ -79,6 +80,7 @@
         )
 
     each(peers - 1, greet)
+    pl.semaphore_signal(barrier, 1, device_id=partner, device_id_type=MESH)
     for load in loads:
         load.wait()
 
@@ -207,17 +209,20 @@
         return recv1.at[h, 0, 0, pl.ds(0, REACH * BAND)]
 
     def sent2(turn):
-        return recv2.at[pl.ds(0, PEERS - 2), pl.ds(0, COLS if turn == 0 else COLS // 2)]
-
-    project(0, 0)
-    pl.semaphore_wait(barrier, peers - 1)
-    give1(0, 0)
-    project(0, 1)
-    give1(0, 1)
-    project(1, 0)
-    give1(1, 0)
-    project(1, 1)
-    give1(1, 1)
+        count = COLS if turn == 0 else PIECES[turn - 1][1]
+        return recv2.at[pl.ds(0, PEERS - 2), pl.ds(0, count)]
+
+    project(0, core)
+    pl.semaphore_wait(barrier, peers)
+    pl.semaphore_signal(near, 1, device_id=partner, device_id_type=MESH)
+    give1(0, core)
+    project(0, 1 - core)
+    pl.semaphore_wait(near, 1)
+    give1(0, 1 - core)
+    project(1, core)
+    give1(1, core)
+    project(1, 1 - core)
+    give1(1, 1 - core)
     for h in range(2):
         for side in range(2):
             place1(h, side)[...] = send1[h, set_of(core, n, z, side)]
@@ -249,20 +254,19 @@
             if h == 0:
                 give2(0, side, 0, 0, COLS)
         if h == 1:
-            for part in range(2):
+            for turn, (first, count) in enumerate(PIECES):
                 for side in range(2):
-                    give2(1, side, 1 + part, part * (COLS // 2), COLS // 2)
-
-    half = COLS // 2
+                    give2(1, side, 1 + turn, first, count)
+
     wait_for(sent2(0), rsem2.at[0])
-    for part in range(2):
-        wait_for(sent2(1 + part), rsem2.at[1 + part])
-        here = pl.ds(part * half, half)
+    for turn, (first, count) in enumerate(PIECES):
+        wait_for(sent2(1 + turn), rsem2.at[1 + turn])
+        here = pl.ds(first, count)
 
         def add(d, c):
             return c + recv2[d, here, :].astype(F32)
 
-        zero = jnp.zeros((half, ROWS), F32)
+        zero = jnp.zeros((count, ROWS), F32)
         mean = lax.fori_loop(0, WIDTH, add, zero, unroll=8) * (1.0 / WIDTH)
 
         def square(d, c):
@@ -275,12 +279,12 @@
 
         def spread(d):
             v = (recv2[d, here, :].astype(F32) - mean) * scale
-            stage[pl.ds(d * S + part * half, half), :] = v
+            stage[pl.ds(d * S + first, count), :] = v
 
         each(WIDTH, spread, 8)
 
         def finish(jj):
-            j = part * (half // 2) + jj
+            j = first // 2 + jj
             s = [
                 (stage[pl.ds(2 * j + t, WIDTH, stride=S), :] * gmid[...]).astype(BF16)
                 for t in range(2)
@@ -290,10 +294,10 @@
             for t in range(2):
                 rows[pl.ds(2 * j + t, ROWS, stride=S), :] = y[:, t * ROWS : (t + 1) * ROWS].T
 
-        each(half // 2, finish, 2)
+        each(count // 2, finish, 2)
 
         def narrow(i):
-            o_ref[i, here, :] = rows[pl.ds(i * S + part * half, half), :].astype(BF16)
+            o_ref[i, here, :] = rows[pl.ds(i * S + first, count), :].astype(BF16)
 
         each(ROWS, narrow, 8)
 
@@ -301,13 +305,15 @@
         wait_for(sent1(h, PEERS - 2), ssem1.at[h])
         for side in range(2):
             wait_for(handed(h), ssemh.at[h, side])
-    for turn in range(3):
+    for turn in range(1 + len(PIECES)):
         wait_for(sent2(turn), ssem2.at[turn])
 
 
 def body(x, in_gain, lw, rw, lg, rg, mid_gain, ow, og):
     vmem = pl.BlockSpec(memory_space=pltpu.VMEM)
     hbm = pl.BlockSpec(memory_space=pltpu.HBM)
+    operands = x, in_gain.reshape(1, WIDTH), lw, rw, lg, rg, mid_gain.reshape(1, WIDTH), ow, og
+    operands = [pltpu.with_memory_space_constraint(a, pltpu.HBM) for a in operands]
     return pl.pallas_call(
         kernel,
         out_shape=jax.ShapeDtypeStruct(x.shape, BF16),
@@ -331,18 +337,19 @@
             pltpu.VMEM((2, 2, REACH * BAND, LINES), BF16),
             pltpu.VMEM((WIDTH, COLS, ROWS), BF16),
             pltpu.SemaphoreType.DMA((9,)),
+            pltpu.SemaphoreType.REGULAR,
             pltpu.SemaphoreType.DMA((2,)),
             pltpu.SemaphoreType.DMA((2, 2)),
             pltpu.SemaphoreType.DMA((2, 2)),
             pltpu.SemaphoreType.DMA((2, 2)),
-            pltpu.SemaphoreType.DMA((3,)),
-            pltpu.SemaphoreType.DMA((3,)),
+            pltpu.SemaphoreType.DMA((1 + len(PIECES),)),
+            pltpu.SemaphoreType.DMA((1 + len(PIECES),)),
         ],
         compiler_params=pltpu.CompilerParams(
-            collective_id=0, has_side_effects=True, vmem_limit_bytes=64_000_000
+            collective_id=0, has_side_effects=True, vmem_limit_bytes=48_000_000
         ),
         name="triangle",
-    )(x, in_gain.reshape(1, WIDTH), lw, rw, lg, rg, mid_gain.reshape(1, WIDTH), ow, og)
+    )(*operands)
 
 
 def solution(mesh):

time: 83.6 us -> 80.6 us (0.964)
  Pallas kernels: 80.2 us -> 78.6 us
  local copies, waits for them, and re-layouts: 2.26 us -> 0.97 us
    pallas_call x1, Pallas kernels: 80.2 us -> 78.6 us  [body(): pl.pallas_call(kernel, out_shape=jax.ShapeDtypeStruct(x.shape, BF16), in_...]
    unnamed x1, local copies, waits for them, and re-layouts: 2.26 us -> 0.97 us
where the time goes in v5:
time: 80.6 us; the launch traced here: 79.5 us
  Pallas kernels  78.6 us (98%)
  local copies, waits for them, and re-layouts  0.97 us (1%)
    pallas_call x1, Pallas kernels, body(): pl.pallas_call(kernel, out_shape=jax.ShapeDtypeStruct(x.shape, BF16), in_...  78.6 us

profile of v5, /device:TPU:7, one launch (start us, length us, event | category | flops | bytes accessed | tf_op | source)
XLA Modules:
  0.0 79.5 jit_solution(3067814411099714583)
XLA Ops:
  0.0 78.6 %triangle.1 = bf16[128,32,128]{2,1,0:T(8,128)(2,1)S(1)} custom-call(bf16[128,32,128]{2,1,0:T(8,128)(2,1)} %x_hbm.1, f32[1,128]{1,0:T(1,128)} %bitcast.2, bf16[128,128]{1,0:T(8,128)(2,1)} %lw_hbm.1, bf16[128,128]{1,0:T(8,128)(2,1)} %rw_hbm.1, bf16[128,128]{1,0:T(8,128)(2,1)} %lg_hbm.1, bf16[128,128]{1,0:T(8,128)(2,1)} %rg_hbm.1, f32[1,128]{1,0:T(1,128)} %bitcast.3, ...), custom_call_target="tpu_custom_call" | custom-call | tf_op jit(solution)/shard_map/triangle/pallas_call | solution.py:317
  78.6 1.0 %copy.11 = bf16[128,32,128]{2,1,0:T(8,128)(2,1)} copy(bf16[128,32,128]{2,1,0:T(8,128)(2,1)S(1)} %triangle.1) | data formatting | bytes 2097152

commit v6 on v5

--- a/solution.py
+++ b/solution.py
@@ -98,7 +98,7 @@
     def widen(k):
         rows[pl.ds(k * S, COLS), :] = x_ref[k].astype(F32)
 
-    each(ROWS, widen, 4)
+    each(ROWS, widen, 16)
 
     def norm(i):
         v = rows[pl.ds(i, ROWS, stride=S), :].T
@@ -106,7 +106,7 @@
         v = v * lax.rsqrt(jnp.mean(v * v, axis=0, keepdims=True) + 1e-05) * gin[...]
         xt[:, pl.ds(pl.multiple_of(i * ROWS, ROWS), ROWS)] = v.astype(BF16)
 
-    each(COLS, norm, 2)
+    each(COLS, norm, 16)
 
     def columns(i):
         return pl.ds(pl.multiple_of(i * 2 * ROWS, 2 * ROWS), 2 * ROWS)
@@ -124,7 +124,7 @@
                         :, t * ROWS : (t + 1) * ROWS
                     ]
 
-        each(COLS // 2, pair, 2)
+        each(COLS // 2, pair, 16)
 
         def pack(p):
             for kind in range(2):
@@ -132,7 +132,7 @@
                     pl.ds((kind * GROUP + p) * S, COLS), :
                 ].astype(BF16)
 
-        each(GROUP, pack, 4)
+        each(GROUP, pack, 16)
 
     def place1(h, side):
         return recv1.at[
@@ -231,7 +231,7 @@
         y = jnp.dot(ogt[...], xt[:, columns(i)], preferred_element_type=F32)
         gate[:, columns(i)] = logistic(y)
 
-    each(COLS // 2, open_gate)
+    each(COLS // 2, open_gate, 4)
 
     for h in range(2):
         for side in range(2):
@@ -267,21 +267,21 @@
             return c + recv2[d, here, :].astype(F32)
 
         zero = jnp.zeros((count, ROWS), F32)
-        mean = lax.fori_loop(0, WIDTH, add, zero, unroll=8) * (1.0 / WIDTH)
+        mean = lax.fori_loop(0, WIDTH, add, zero, unroll=16) * (1.0 / WIDTH)
 
         def square(d, c):
             v = recv2[d, here, :].astype(F32) - mean
             return c + v * v
 
         scale = lax.rsqrt(
-            lax.fori_loop(0, WIDTH, square, zero, unroll=8) * (1.0 / WIDTH) + 1e-05
+            lax.fori_loop(0, WIDTH, square, zero, unroll=16) * (1.0 / WIDTH) + 1e-05
         )
 
         def spread(d):
             v = (recv2[d, here, :].astype(F32) - mean) * scale
             stage[pl.ds(d * S + first, count), :] = v
 
-        each(WIDTH, spread, 8)
+        each(WIDTH, spread, 16)
 
         def finish(jj):
             j = first // 2 + jj
@@ -294,12 +294,12 @@
             for t in range(2):
                 rows[pl.ds(2 * j + t, ROWS, stride=S), :] = y[:, t * ROWS : (t + 1) * ROWS].T
 
-        each(count // 2, finish, 2)
+        each(count // 2, finish, 4)
 
         def narrow(i):
             o_ref[i, here, :] = rows[pl.ds(i * S + first, count), :].astype(BF16)
 
-        each(ROWS, narrow, 8)
+        each(ROWS, narrow, 16)
 
     for h in range(2):
         wait_for(sent1(h, PEERS - 2), ssem1.at[h])

time: 80.6 us -> 77.5 us (0.962)
  Pallas kernels: 78.6 us -> 76.1 us
    pallas_call x1, Pallas kernels: 78.6 us -> 76.1 us  [body(): pl.pallas_call(kernel, out_shape=jax.ShapeDtypeStruct(x.shape, BF16), in_...]
where the time goes in v6:
time: 77.5 us; the launch traced here: 77 us
  Pallas kernels  76.1 us (98%)
  local copies, waits for them, and re-layouts  0.97 us (1%)
    pallas_call x1, Pallas kernels, body(): pl.pallas_call(kernel, out_shape=jax.ShapeDtypeStruct(x.shape, BF16), in_...  76.1 us

profile of v6, /device:TPU:7, one launch (start us, length us, event | category | flops | bytes accessed | tf_op | source)
XLA Modules:
  0.0 77.0 jit_solution(2618908318215286001)
XLA Ops:
  0.0 76.1 %triangle.1 = bf16[128,32,128]{2,1,0:T(8,128)(2,1)S(1)} custom-call(bf16[128,32,128]{2,1,0:T(8,128)(2,1)} %x_hbm.1, f32[1,128]{1,0:T(1,128)} %bitcast.2, bf16[128,128]{1,0:T(8,128)(2,1)} %lw_hbm.1, bf16[128,128]{1,0:T(8,128)(2,1)} %rw_hbm.1, bf16[128,128]{1,0:T(8,128)(2,1)} %lg_hbm.1, bf16[128,128]{1,0:T(8,128)(2,1)} %rg_hbm.1, f32[1,128]{1,0:T(1,128)} %bitcast.3, ...), custom_call_target="tpu_custom_call" | custom-call | tf_op jit(solution)/shard_map/triangle/pallas_call | solution.py:317
  76.1 1.0 %copy.11 = bf16[128,32,128]{2,1,0:T(8,128)(2,1)} copy(bf16[128,32,128]{2,1,0:T(8,128)(2,1)S(1)} %triangle.1) | data formatting | bytes 2097152

commit v7 on v6

--- a/solution.py
+++ b/solution.py
@@ -37,7 +37,7 @@
 def kernel(
     x_hbm, in_gain_hbm, lw_hbm, rw_hbm, lg_hbm, rg_hbm, mid_gain_hbm, ow_hbm, og_hbm, o_ref,
     x_ref, weights, gains, rows, xt, gate, stage, wt, owt, ogt, gin, gmid,
-    send1, recv1, send2, recv2, lsem, near, ssem1, rsem1, ssemh, rsemh, ssem2, rsem2,
+    send1, recv1, send2, recv2, lsem, near_row, near, ssem1, rsem1, ssemh, rsemh, ssem2, rsem2,
 ):
     n, e = lax.axis_index("north"), lax.axis_index("east")
     z, core = e // CORES, lax.rem(e, CORES)
@@ -60,28 +60,36 @@
         loads.append(pltpu.make_async_copy(w, weights.at[i], lsem.at[1 + i]))
     for i, g in enumerate((in_gain_hbm, mid_gain_hbm)):
         loads.append(pltpu.make_async_copy(g, gains.at[i], lsem.at[7 + i]))
-    for load in loads:
-        load.start()
+    loads[0].start()
 
     barrier = pltpu.get_barrier_semaphore()
     partner = {"north": n, "east": e + 1 - 2 * core}
-    peers = (2 * REACH - 1) * NORTH
-
-    def greet(s):
-        q = peers - 1 - s
-        far = q // NORTH
-        step = (far + 1) // 2 * (1 - 2 * lax.rem(far, 2))
+    in_row = 2 * (REACH - 1)
+
+    def greet_row(s):
+        step = (REACH - 1 - s // 2) * (1 - 2 * lax.rem(s, 2))
         e2 = lax.rem(z + CHIPS + step, CHIPS) * CORES + core
         pl.semaphore_signal(
-            barrier,
-            1,
-            device_id={"north": lax.rem(n + q, NORTH), "east": e2},
-            device_id_type=MESH,
+            barrier, 1, device_id={"north": n, "east": e2}, device_id_type=MESH
         )
 
-    each(peers - 1, greet)
+    def greet_column(sem):
+        def go(s):
+            pl.semaphore_signal(
+                sem,
+                1,
+                device_id={"north": lax.rem(n + s, NORTH), "east": e},
+                device_id_type=MESH,
+            )
+
+        each(NORTH, go, start=1)
+
+    each(in_row, greet_row)
+    greet_column(barrier)
     pl.semaphore_signal(barrier, 1, device_id=partner, device_id_type=MESH)
-    for load in loads:
+    for load in loads[1:]:
+        load.start()
+    for load in loads[1:]:
         load.wait()
 
     for kind in range(4):
@@ -95,6 +103,8 @@
     gin[...] = column(gains[0])
     gmid[...] = column(gains[1])
 
+    loads[0].wait()
+
     def widen(k):
         rows[pl.ds(k * S, COLS), :] = x_ref[k].astype(F32)
 
@@ -106,12 +116,11 @@
         v = v * lax.rsqrt(jnp.mean(v * v, axis=0, keepdims=True) + 1e-05) * gin[...]
         xt[:, pl.ds(pl.multiple_of(i * ROWS, ROWS), ROWS)] = v.astype(BF16)
 
-    each(COLS, norm, 16)
 
     def columns(i):
         return pl.ds(pl.multiple_of(i * 2 * ROWS, 2 * ROWS), 2 * ROWS)
 
-    def project(h, c):
+    def project(h, c, lo=0, hi=COLS):
         def pair(i):
             y = jnp.dot(
                 wt[h, c].reshape(4 * GROUP, WIDTH), xt[:, columns(i)], preferred_element_type=F32
@@ -124,40 +133,41 @@
                         :, t * ROWS : (t + 1) * ROWS
                     ]
 
-        each(COLS // 2, pair, 16)
+        each(hi // 2, pair, (hi - lo) // 2, start=lo // 2)
 
         def pack(p):
             for kind in range(2):
-                send1[h, c * GROUP + p, kind] = stage[
-                    pl.ds((kind * GROUP + p) * S, COLS), :
+                send1[h, c * GROUP + p, kind, lo:hi] = stage[
+                    pl.ds((kind * GROUP + p) * S + lo, hi - lo), :
                 ].astype(BF16)
 
         each(GROUP, pack, 16)
 
-    def place1(h, side):
+    def place1(h, side, lo=0, hi=COLS):
         return recv1.at[
             h,
             side,
             :,
-            pl.ds(pl.multiple_of(e * COLS, COLS), COLS),
+            pl.ds(pl.multiple_of(e * COLS + lo, hi - lo), hi - lo),
             pl.ds(pl.multiple_of(n * ROWS, ROWS), ROWS),
         ]
 
-    def give1(h, c):
+    def give1(h, c, first=0, count=NORTH, lo=0, hi=COLS):
         def go(s):
-            q = GROUP - 1 - s
-            side, n2, steps = lax.rem(q, 2), lax.rem(n + q // 2, NORTH), q // (2 * NORTH)
+            side, steps = lax.rem(s, 2), REACH - 1 - s // (2 * count)
+            n2 = lax.rem(n + first + count - 1 - lax.rem(s // 2, count), NORTH)
             z2 = away(1 - side, steps)
             pltpu.make_async_remote_copy(
-                send1.at[h, set_of(c, n2, z2, side)],
-                place1(h, side),
+                send1.at[h, set_of(c, n2, z2, side), :, pl.ds(lo, hi - lo)],
+                place1(h, side, lo, hi),
                 ssem1.at[h],
                 rsem1.at[h, side],
                 device_id={"north": n2, "east": z2 * CORES + c},
                 device_id_type=MESH,
             ).start()
 
-        each(GROUP - 2 * (1 - lax.rem(c + core, CORES)), go)
+        own = 0 if first else 2 * (1 - lax.rem(c + core, CORES))
+        each(REACH * 2 * count - own, go)
 
     def band(h, side, kind, steps):
         first = pl.multiple_of(away(side, steps) * BAND, BAND)
@@ -212,10 +222,18 @@
         count = COLS if turn == 0 else PIECES[turn - 1][1]
         return recv2.at[pl.ds(0, PEERS - 2), pl.ds(0, count)]
 
-    project(0, core)
-    pl.semaphore_wait(barrier, peers)
+    half = COLS // 2
+    each(half, norm, half)
+    project(0, core, 0, half)
+    pl.semaphore_wait(barrier, in_row + NORTH)
+    greet_column(near_row)
+    give1(0, core, 0, 1, 0, half)
+    each(COLS, norm, half, start=half)
+    project(0, core, half, COLS)
+    pl.semaphore_wait(near_row, NORTH - 1)
     pl.semaphore_signal(near, 1, device_id=partner, device_id_type=MESH)
-    give1(0, core)
+    give1(0, core, 1, NORTH - 1, 0, half)
+    give1(0, core, 0, NORTH, half, COLS)
     project(0, 1 - core)
     pl.semaphore_wait(near, 1)
     give1(0, 1 - core)
@@ -263,18 +281,23 @@
         wait_for(sent2(1 + turn), rsem2.at[1 + turn])
         here = pl.ds(first, count)
 
+        def tree(v):
+            while v.shape[0] > 1:
+                v = v[: v.shape[0] // 2] + v[v.shape[0] // 2 :]
+            return v[0]
+
         def add(d, c):
-            return c + recv2[d, here, :].astype(F32)
+            return c + tree(recv2[pl.ds(d * 16, 16), here, :].astype(F32))
 
         zero = jnp.zeros((count, ROWS), F32)
-        mean = lax.fori_loop(0, WIDTH, add, zero, unroll=16) * (1.0 / WIDTH)
+        mean = lax.fori_loop(0, WIDTH // 16, add, zero, unroll=2) * (1.0 / WIDTH)
 
         def square(d, c):
-            v = recv2[d, here, :].astype(F32) - mean
-            return c + v * v
+            v = recv2[pl.ds(d * 16, 16), here, :].astype(F32) - mean
+            return c + tree(v * v)
 
         scale = lax.rsqrt(
-            lax.fori_loop(0, WIDTH, square, zero, unroll=16) * (1.0 / WIDTH) + 1e-05
+            lax.fori_loop(0, WIDTH // 16, square, zero, unroll=2) * (1.0 / WIDTH) + 1e-05
         )
 
         def spread(d):
@@ -338,6 +361,7 @@
             pltpu.VMEM((WIDTH, COLS, ROWS), BF16),
             pltpu.SemaphoreType.DMA((9,)),
             pltpu.SemaphoreType.REGULAR,
+            pltpu.SemaphoreType.REGULAR,
             pltpu.SemaphoreType.DMA((2,)),
             pltpu.SemaphoreType.DMA((2, 2)),
             pltpu.SemaphoreType.DMA((2, 2)),

time: 77.5 us -> 76.8 us (level)
  Pallas kernels: 76.1 us -> 74.9 us
    pallas_call x1, Pallas kernels: 76.1 us -> 74.9 us  [body(): pl.pallas_call(kernel, out_shape=jax.ShapeDtypeStruct(x.shape, BF16), in_...]
where the time goes in v7:
time: 76.8 us; the launch traced here: 75.8 us
  Pallas kernels  74.9 us (98%)
  local copies, waits for them, and re-layouts  0.97 us (1%)
    pallas_call x1, Pallas kernels, body(): pl.pallas_call(kernel, out_shape=jax.ShapeDtypeStruct(x.shape, BF16), in_...  74.9 us

profile of v7, /device:TPU:7, one launch (start us, length us, event | category | flops | bytes accessed | tf_op | source)
XLA Modules:
  0.0 75.8 jit_solution(16180136953130962575)
XLA Ops:
  0.0 74.9 %triangle.1 = bf16[128,32,128]{2,1,0:T(8,128)(2,1)S(1)} custom-call(bf16[128,32,128]{2,1,0:T(8,128)(2,1)} %x_hbm.1, f32[1,128]{1,0:T(1,128)} %bitcast.2, bf16[128,128]{1,0:T(8,128)(2,1)} %lw_hbm.1, bf16[128,128]{1,0:T(8,128)(2,1)} %rw_hbm.1, bf16[128,128]{1,0:T(8,128)(2,1)} %lg_hbm.1, bf16[128,128]{1,0:T(8,128)(2,1)} %rg_hbm.1, f32[1,128]{1,0:T(1,128)} %bitcast.3, ...), custom_call_target="tpu_custom_call" | custom-call | tf_op jit(solution)/shard_map/triangle/pallas_call | solution.py:340
  74.9 1.0 %copy.11 = bf16[128,32,128]{2,1,0:T(8,128)(2,1)} copy(bf16[128,32,128]{2,1,0:T(8,128)(2,1)S(1)} %triangle.1) | data formatting | bytes 2097152
